TPU v7x, 32 devices: a whole 2x2x4 slice. The times are simulated.
32 devices in a mesh: row: 8 (over z, y), col: 4 (over x, core).
Axes of the slice: x: 2, y: 2, z: 4, core: 2. Of those that a mesh axis runs over, the one named last changes fastest.
Arguments:
- tracer: float32 [128, 128, 512], P(None, 'row', 'col'), may hold values from -6 to 6
- symbol_x: float32 [128], replicated, may hold values from 0.3 to 3
- symbol_y: float32 [128], replicated, may hold values from 0.3 to 3
- symbol_z: float32 [512], replicated, may hold values from 0.3 to 3
Outputs:
- spectrum: float32 [128, 128, 512], P('row', 'col')
All inputs are finite; a program needn't handle non-finite values.
Results may differ from a plain program's by a relative error of at most 0.000075.
Values sent between devices are 32-bit elements; how exact they have to be, the bound alone decides.
No kernel may reach another device: no remote copies, remote signals or barrier semaphores. Data moves between devices by JAX's collectives and lax.ppermute only.
A program may use at most 64 MiB of HBM per device.

v0:
```python
import jax
import jax.numpy as jnp
from jax import lax
from jax.sharding import PartitionSpec as P


def transform_table(count):
    rank = jnp.arange(count)
    angle = (
        jnp.pi
        / (count + 1)
        * ((rank[:, None] + 1) * (rank[None, :] + 1) % (2 * count + 2)).astype(jnp.float32)
    )
    return jnp.sin(angle) * (2.0 / (count + 1)) ** 0.5


def to_modes(values, dim):
    moved = jnp.tensordot(
        values,
        transform_table(values.shape[dim]),
        axes=([dim], [0]),
        precision=lax.Precision.HIGHEST,
    )
    return jnp.moveaxis(moved, -1, dim)


def per_device(tracer, symbol_x, symbol_y, symbol_z):
    part_values = tracer
    part_values = to_modes(part_values, 0)
    part_values = lax.all_to_all(part_values, "row", split_axis=0, concat_axis=1, tiled=True)
    part_values = to_modes(part_values, 1)
    local_values = part_values
    local_values = lax.all_to_all(local_values, "col", split_axis=1, concat_axis=2, tiled=True)
    local_values = to_modes(local_values, 2)
    share_x = local_values.shape[0]
    part_x = lax.dynamic_slice_in_dim(symbol_x, lax.axis_index("row") * share_x, share_x)
    share_y = local_values.shape[1]
    part_y = lax.dynamic_slice_in_dim(symbol_y, lax.axis_index("col") * share_y, share_y)
    symbol = part_x[:, None, None] + part_y[None, :, None] + symbol_z[None, None, :]
    local_values = local_values * ((1.0 - 0.2 * symbol) / (1.0 + 0.2 * symbol))
    return local_values


def solution(mesh):
    in_specs = (P(None, "row", "col"), P(), P(), P())
    out_specs = P("row", "col", None)
    return jax.shard_map(
        per_device, mesh=mesh, in_specs=in_specs, out_specs=out_specs, check_vma=False
    )
```

profile of v0, /device:TPU:0, one launch (start us, length us, event | category | flops | bytes accessed | tf_op | source)
XLA Modules:
  0.0 66.0 jit_solution(14999294112049493810)
XLA Ops:
  0.0 0.0 copy-start
  0.0 1.2 %copy-done = f32[128,16,128]{2,1,0:T(8,128)S(1)} copy-done((f32[128,16,128]{2,1,0:T(8,128)S(1)}, f32[128,16,128]{2,1,0:T(8,128)}, u32[]{:S(2)}) %copy-start) | copy-done | bytes 1048600
  1.2 1.6 %fusion.6 = f32[128,16,128]{2,0,1:T(8,128)S(1)} fusion(f32[128,16,128]{2,1,0:T(8,128)S(1)} %copy-done, s32[128]{0:T(128)S(1)} %iota_add_fusion.1), kind=kOutput, calls=%fused_computation.8 | convolution fusion | flops 402817024 | bytes 2097664 | tf_op jit(solution)/shard_map/dot_general | solution.py:18
  2.8 0.6 copy.24
  3.5 32.9 %all_to_all.36 = f32[128,16,128]{2,1,0:T(8,128)S(1)} all-to-all(f32[128,16,128]{2,1,0:T(8,128)S(1)} %copy.24), channel_id=1, replica_groups=mesh['row'=8,'col'=4] {'row'}, dimensions={0} | all-to-all | bytes 2097152 | tf_op jit(solution)/shard_map/all_to_all | solution.py:30
  36.3 0.1 copy.25
  36.4 2.0 %convolution_bitcast_fusion = f32[16,128,128]{1,2,0:T(8,128)S(1)} fusion(f32[16,128,128]{2,1,0:T(8,128)S(1)} %bitcast.21, s32[128]{0:T(128)S(1)} %iota_add_fusion.1), kind=kOutput, calls=%fused_computation.2 | convolution fusion | flops 402817024 | bytes 2097664 | tf_op jit(solution)/shard_map/dot_general | solution.py:18
  38.4 1.4 %copy.27 = f32[16,128,128]{2,0,1:T(8,128)} copy(f32[16,128,128]{1,2,0:T(8,128)S(1)} %convolution_bitcast_fusion) | data formatting | bytes 2097152 | tf_op jit(solution)/shard_map/transpose | solution.py:24
  39.8 3.7 %all-to-all-start.1 = ((f32[16,128,128]{2,0,1:T(8,128)}), f32[16,128,128]{2,0,1:T(8,128)S(1)}, u32[]{:S(2)}, u32[]{:S(2)}) async-start(f32[16,128,128]{2,0,1:T(8,128)} %copy.27), calls=%async_computation.1 | async-start | bytes 2097152 | tf_op jit(solution)/shard_map/all_to_all | solution.py:33
  43.5 0.0 copy-start.2
  43.5 0.6 copy-done.2
  44.2 0.1 dynamic_slice.7
  44.2 0.0 copy-start.3
  44.2 0.7 copy-done.3
  44.9 0.1 dynamic_slice.6
  45.0 0.1 broadcast_add_fusion
  45.0 12.7 %all-to-all-done.1 = f32[16,128,128]{2,0,1:T(8,128)S(1)} async-done(((f32[16,128,128]{2,0,1:T(8,128)}), f32[16,128,128]{2,0,1:T(8,128)S(1)}, u32[]{:S(2)}, u32[]{:S(2)}) %all-to-all-start.1) | async-done | bytes 1048608 | tf_op jit(solution)/shard_map/all_to_all | solution.py:33
  57.7 0.7 %copy.29 = f32[16,32,4,128]{3,2,1,0:T(4,128)S(1)} copy(f32[16,32,4,128]{3,0,1,2:T(8,128)S(1)} %bitcast.19) | data formatting | bytes 2097152 | tf_op jit(solution)/shard_map/all_to_all | solution.py:33
  58.4 0.0 copy-start.1
  58.4 0.4 all_to_all.33
  58.8 0.2 copy-done.1
  59.1 7.0 %convolution_multiply_fusion = f32[16,32,512]{2,1,0:T(8,128)} fusion(f32[16,32,512]{2,1,0:T(8,128)S(1)} %all_to_all.33, f32[512]{0:T(512)S(1)} %copy-done.1, f32[16,32]{1,0:T(8,128)S(1)} %broadcast_add_fusion, s32[512]{0:T(512)S(1)} %iota_add_fusion), kind=kOutput, calls=%fused_computation.1 | convolution fusion | flops 1614807040 | bytes 2103296 | tf_op jit(solution)/shard_map/dot_general | solution.py:18
  (2 shorter events, 0.0 us)
Async XLA Ops:
  0.0 1.2 %copy-start = (f32[128,16,128]{2,1,0:T(8,128)S(1)}, f32[128,16,128]{2,1,0:T(8,128)}, u32[]{:S(2)}) copy-start(f32[128,16,128]{2,1,0:T(8,128)} %param.4) | copy-start | bytes 3145732
  39.8 17.9 %all-to-all-start.1 = ((f32[16,128,128]{2,0,1:T(8,128)}), f32[16,128,128]{2,0,1:T(8,128)S(1)}, u32[]{:S(2)}, u32[]{:S(2)}) async-start(f32[16,128,128]{2,0,1:T(8,128)} %copy.27), calls=%async_computation.1 | async-start | bytes 2097152 | tf_op jit(solution)/shard_map/all_to_all | solution.py:33
  43.5 0.7 copy-start.2
  44.2 0.7 copy-start.3
  58.4 0.7 %copy-start.1 = (f32[512]{0:T(512)S(1)}, f32[512]{0:T(512)}, u32[]{:S(2)}) copy-start(f32[512]{0:T(512)} %param.7) | copy-start | bytes 6148
where the time goes:
time: 66.3 us; the launch traced here: 66 us
  blocking collectives  32.9 us (50%)
  waiting for transfers between devices  12.7 us (19%)
  matrix products  10.5 us (16%)
  local copies, waits for them, and re-layouts  6.11 us (9%)
  starting transfers between devices  3.7 us (6%)
    all_to_all x1, blocking collectives, per_device(): lax.all_to_all(part_values, 'row', split_axis=0, concat_axis=1, tiled=True)  32.9 us
    all_to_all x1, waiting for transfers between devices, per_device(): lax.all_to_all(local_values, 'col', split_axis=1, concat_axis=2, tiled=True)  12.7 us
    dot_general x3, matrix products, to_modes(): jnp.tensordot(values, transform_table(values.shape[dim]), axes=([dim], [0...  10.5 us
    all_to_all x1, starting transfers between devices, per_device(): lax.all_to_all(local_values, 'col', split_axis=1, concat_axis=2, tiled=True)  3.7 us
    unnamed x8, local copies, waits for them, and re-layouts  2.77 us
    transpose x1, local copies, waits for them, and re-layouts, to_modes(): return jnp.moveaxis(moved, -1, dim)  1.38 us
  transfers between devices with their start and end apart: 1, of which 1 were waited for; matrix products, arithmetic and copies ran while one was open for 0% of the time, Pallas kernels for 0%

commit v1 on v0

--- a/solution.py
+++ b/solution.py
@@ -30,7 +30,9 @@
     part_values = lax.all_to_all(part_values, "row", split_axis=0, concat_axis=1, tiled=True)
     part_values = to_modes(part_values, 1)
     local_values = part_values
-    local_values = lax.all_to_all(local_values, "col", split_axis=1, concat_axis=2, tiled=True)
+    cells = jnp.split(local_values, lax.axis_size("col"), axis=1)
+    received = lax.all_to_all(jnp.stack(cells), "col", 0, 0)
+    local_values = jnp.concatenate(received, axis=2)
     local_values = to_modes(local_values, 2)
     share_x = local_values.shape[0]
     part_x = lax.dynamic_slice_in_dim(symbol_x, lax.axis_index("row") * share_x, share_x)

time: 66.3 us -> 64.2 us (0.968)
  local copies, waits for them, and re-layouts: 6.11 us -> 3.48 us
  other arithmetic: 0.08 us -> 1.12 us
    transpose x1 -> x0, local copies, waits for them, and re-layouts: 1.38 us -> none  [to_modes(): return jnp.moveaxis(moved, -1, dim)]
    all_to_all x2 -> x0, local copies, waits for them, and re-layouts: 1.1 us -> none  [per_device(): lax.all_to_all(local_values, 'col', split_axis=1, concat_axis=2, tiled=True)]
    another operation x0 -> x1, other arithmetic: none -> 1.04 us  [per_device(): received = lax.all_to_all(jnp.stack(cells), 'col', 0, 0)]
where the time goes in v1:
time: 64.2 us; the launch traced here: 63.9 us
  blocking collectives  32.9 us (51%)
  waiting for transfers between devices  12.9 us (20%)
  matrix products  9.99 us (16%)
  starting transfers between devices  3.52 us (5%)
  local copies, waits for them, and re-layouts  3.48 us (5%)
  other arithmetic  1.12 us (2%)
    all_to_all x1, blocking collectives, per_device(): lax.all_to_all(part_values, 'row', split_axis=0, concat_axis=1, tiled=True)  32.9 us
    all_to_all x1, waiting for transfers between devices, per_device(): received = lax.all_to_all(jnp.stack(cells), 'col', 0, 0)  12.9 us
    dot_general x3, matrix products, to_modes(): jnp.tensordot(values, transform_table(values.shape[dim]), axes=([dim], [0...  9.99 us
    all_to_all x1, starting transfers between devices, per_device(): received = lax.all_to_all(jnp.stack(cells), 'col', 0, 0)  3.52 us
    unnamed x8, local copies, waits for them, and re-layouts  2.53 us
  transfers between devices with their start and end apart: 1, of which 1 were waited for; matrix products, arithmetic and copies ran while one was open for 0% of the time, Pallas kernels for 0%

profile of v1, /device:TPU:0, one launch (start us, length us, event | category | flops | bytes accessed | tf_op | source)
XLA Modules:
  0.0 63.9 jit_solution(8312727418267081878)
XLA Ops:
  0.0 0.0 copy-start
  0.0 1.2 %copy-done = f32[128,16,128]{2,1,0:T(8,128)S(1)} copy-done((f32[128,16,128]{2,1,0:T(8,128)S(1)}, f32[128,16,128]{2,1,0:T(8,128)}, u32[]{:S(2)}) %copy-start) | copy-done | bytes 1048600
  1.2 1.6 %fusion.8 = f32[128,16,128]{2,0,1:T(8,128)S(1)} fusion(f32[128,16,128]{2,1,0:T(8,128)S(1)} %copy-done, s32[128]{0:T(128)S(1)} %iota_add_fusion.1), kind=kOutput, calls=%fused_computation.11 | convolution fusion | flops 402817024 | bytes 2097664 | tf_op jit(solution)/shard_map/dot_general | solution.py:18
  2.8 0.6 copy.11
  3.4 32.9 %all_to_all.23 = f32[128,16,128]{2,1,0:T(8,128)S(1)} all-to-all(f32[128,16,128]{2,1,0:T(8,128)S(1)} %copy.11), channel_id=1, replica_groups=mesh['row'=8,'col'=4] {'row'}, dimensions={0} | all-to-all | bytes 2097152 | tf_op jit(solution)/shard_map/all_to_all | solution.py:30
  36.3 0.1 copy.12
  36.4 1.4 %convolution_bitcast_fusion = f32[16,128,128]{2,1,0:T(8,128)S(1)} fusion(f32[16,128,128]{2,1,0:T(8,128)S(1)} %bitcast.31, s32[128]{0:T(128)S(1)} %iota_add_fusion.1), kind=kOutput, calls=%fused_computation.2 | convolution fusion | flops 402817024 | bytes 2097664 | tf_op jit(solution)/shard_map/dot_general | solution.py:18
  37.9 0.1 slice_bitcast_fusion.3
  38.0 1.0 %pad_maximum_fusion = f32[4,16,32,128]{3,2,1,0:T(8,128)} fusion(f32[1,16,32,128]{3,2,1,0:T(8,128)S(1)} %get-tuple-element.6, f32[1,16,32,128]{3,2,1,0:T(8,128)S(1)} %get-tuple-element.7, f32[1,16,32,128]{3,2,1,0:T(8,128)S(1)} %get-tuple-element.8, f32[1,16,32,128]{3,2,1,0:T(8,128)S(1)} %get-tuple-element.5), kind=kLoop, calls=%fused_computation.10 | loop fusion | flops 786432 | bytes 2097152 | tf_op jit(solution)/shard_map/stack | solution.py:34
  39.0 3.5 %all-to-all-start.1 = ((f32[4,16,32,128]{3,2,1,0:T(8,128)}), f32[4,16,32,128]{3,2,1,0:T(8,128)S(1)}, u32[]{:S(2)}, u32[]{:S(2)}) async-start(f32[4,16,32,128]{3,2,1,0:T(8,128)} %pad_maximum_fusion), calls=%async_computation.1 | async-start | bytes 2097152 | tf_op jit(solution)/shard_map/all_to_all | solution.py:34
  42.5 0.0 copy-start.2
  42.5 0.6 %copy-done.2 = f32[128]{0:T(128)S(1)} copy-done((f32[128]{0:T(128)S(1)}, f32[128]{0:T(128)}, u32[]{:S(2)}) %copy-start.2) | copy-done | bytes 536
  43.2 0.1 dynamic_slice.6
  43.3 0.0 copy-start.3
  43.3 0.7 %copy-done.3 = f32[128]{0:T(128)S(1)} copy-done((f32[128]{0:T(128)S(1)}, f32[128]{0:T(128)}, u32[]{:S(2)}) %copy-start.3) | copy-done | bytes 536
  43.9 0.1 dynamic_slice.7
  44.0 0.0 copy-start.1
  44.0 0.1 broadcast_add_fusion
  44.1 12.9 %all-to-all-done.1 = f32[4,16,32,128]{3,2,1,0:T(8,128)S(1)} async-done(((f32[4,16,32,128]{3,2,1,0:T(8,128)}), f32[4,16,32,128]{3,2,1,0:T(8,128)S(1)}, u32[]{:S(2)}, u32[]{:S(2)}) %all-to-all-start.1) | async-done | bytes 1048608 | tf_op jit(solution)/shard_map/all_to_all | solution.py:34
  56.9 0.0 copy-done.1
  56.9 7.0 %convolution_multiply_fusion = f32[16,32,512]{2,1,0:T(8,128)} fusion(f32[512]{0:T(512)S(1)} %copy-done.1, f32[16,32]{1,0:T(8,128)S(1)} %broadcast_add_fusion, s32[512]{0:T(512)S(1)} %iota_add_fusion, f32[4,16,32,128]{3,2,1,0:T(8,128)S(1)} %all-to-all-done.1), kind=kOutput, calls=%fused_computation.1 | convolution fusion | flops 1614807040 | bytes 2103296 | tf_op jit(solution)/shard_map/dot_general | solution.py:18
  (2 shorter events, 0.0 us)
Async XLA Ops:
  0.0 1.2 %copy-start = (f32[128,16,128]{2,1,0:T(8,128)S(1)}, f32[128,16,128]{2,1,0:T(8,128)}, u32[]{:S(2)}) copy-start(f32[128,16,128]{2,1,0:T(8,128)} %param.4) | copy-start | bytes 3145732
  39.0 17.9 %all-to-all-start.1 = ((f32[4,16,32,128]{3,2,1,0:T(8,128)}), f32[4,16,32,128]{3,2,1,0:T(8,128)S(1)}, u32[]{:S(2)}, u32[]{:S(2)}) async-start(f32[4,16,32,128]{3,2,1,0:T(8,128)} %pad_maximum_fusion), calls=%async_computation.1 | async-start | bytes 2097152 | tf_op jit(solution)/shard_map/all_to_all | solution.py:34
  42.5 0.7 %copy-start.2 = (f32[128]{0:T(128)S(1)}, f32[128]{0:T(128)}, u32[]{:S(2)}) copy-start(f32[128]{0:T(128)} %param.5) | copy-start | bytes 1540
  43.3 0.7 %copy-start.3 = (f32[128]{0:T(128)S(1)}, f32[128]{0:T(128)}, u32[]{:S(2)}) copy-start(f32[128]{0:T(128)} %param.6) | copy-start | bytes 1540
  44.0 12.9 %copy-start.1 = (f32[512]{0:T(512)S(1)}, f32[512]{0:T(512)}, u32[]{:S(2)}) copy-start(f32[512]{0:T(512)} %param.7) | copy-start | bytes 6148
